TPU v7x, 32 devices: a whole 2x2x4 slice. The times are simulated.
32 devices in a mesh: blk: 16 (over z, y, core), head: 2 (over x).
Axes of the slice: x: 2, y: 2, z: 4, core: 2. Of those that a mesh axis runs over, the one named last changes fastest.
Arguments:
- queries: bfloat16 [4096, 1024], P('blk', 'head'), may hold values from -216 to 216
- keys: bfloat16 [4096, 1024], P('blk', 'head'), may hold values from -6 to 6
- values: bfloat16 [4096, 1024], P('blk', 'head'), may hold values from -6 to 6
- group_table: int32 [16, 2], P('blk'), may hold values from 0 to 31, as said below
- doc_ids: int32 [4096], replicated, may hold values from 0 to 15, never falling along the last dimension, each value on 1 to 2048 neighbouring positions
Outputs:
- attended: bfloat16 [4096, 1024], P('blk', 'head')
Inputs may be any that keep to these rules, and one draw needn't show every extreme that they name: group_table[d, 1] = 31 - group_table[d, 0]; the first column holds each of 0 to 15 once. `doc_ids`: document numbers never fall along positions; a document holds at most 2048 positions.
All inputs are finite; a program needn't handle non-finite values.
Results may differ from a plain program's by a relative error of at most 0.0049.
Values may be sent and summed in bfloat16 or wider, within the bound.
A program may use at most 192 MiB of HBM per device.

v0:
```python
import functools
import math

import jax
import jax.numpy as jnp
from jax import lax
from jax.experimental import pallas as pl
from jax.experimental.pallas import tpu as pltpu
from jax.sharding import PartitionSpec as P

HEAD_DIM = 128
CORES = 2
LANES = 2


def attend_kernel(
    line, table_ref, q_hbm, k_hbm, v_hbm, table_hbm, doc_ref, out_ref,
    kv, posb, q_ref, low_ref, high_ref, top, total, acc, recv, precv, send, psend, load,
):
    rows, cols = k_hbm.shape
    heads = cols // HEAD_DIM
    group = rows // 2
    factor = math.log2(math.e) / math.sqrt(HEAD_DIM)
    me = lax.axis_index("blk")
    core = lax.rem(me, CORES)
    lane = lax.rem(me // CORES, LANES)
    z = me // (CORES * LANES)

    def index(zz, yy, cc):
        return (zz * LANES + yy) * CORES + cc

    across = index(z, 1 - lane, core)
    partner = index(z, lane, 1 - core)
    ahead = index(z + 1, lane, core)
    behind = index(z - 1, lane, core)
    has_ahead = z + 1 < line
    has_behind = z >= 1

    short = rows // 8
    half = (rows - short) // 2
    pieces = ((0, short), (short, half), (short + half, half))

    loads = (
        pltpu.make_async_copy(k_hbm, kv.at[me, :, pl.ds(0, cols)], load.at[0]),
        pltpu.make_async_copy(v_hbm, kv.at[me, :, pl.ds(cols, cols)], load.at[1]),
        pltpu.make_async_copy(table_hbm, posb.at[me], load.at[2]),
        pltpu.make_async_copy(q_hbm, q_ref, load.at[3]),
    )
    for one in loads:
        one.start()

    barrier = pltpu.get_barrier_semaphore()

    def greet(target):
        pl.semaphore_signal(barrier, inc=1, device_id={"blk": target})

    greet(across)
    greet(partner)
    pl.when(has_ahead)(lambda: greet(ahead))
    pl.when(has_behind)(lambda: greet(behind))
    pl.semaphore_wait(barrier, 2 + has_ahead.astype(jnp.int32) + has_behind.astype(jnp.int32))

    def remote(src, dst, ssem, rsem, target):
        return pltpu.make_async_remote_copy(
            src_ref=src, dst_ref=dst, send_sem=ssem, recv_sem=rsem, device_id={"blk": target}
        )

    def relay_copies(source, piece, kind, target):
        start, size = pieces[piece]
        part = pl.ds(start, size)
        found = [remote(kv.at[source, part], kv.at[source, part], send.at[source, piece, kind], recv.at[source, piece], target)]
        if piece == 1:
            found.append(remote(posb.at[source], posb.at[source], psend.at[source, kind], precv.at[source], target))
        return found

    def start_all(copies):
        for one in copies:
            one.start()

    def end_sends(copies):
        for one in copies:
            one.wait_send()

    def arrived(source, piece):
        for one in relay_copies(source, piece, 0, partner):
            one.wait_recv()

    def own_routes(act):
        for piece in (0, 1, 2):
            act(relay_copies(me, piece, 2, across))
            pl.when(has_ahead)(lambda: act(relay_copies(me, piece, 0, ahead)))
            pl.when(has_behind)(lambda: act(relay_copies(me, piece, 1, behind)))
            act(relay_copies(me, piece, 3, partner))

    directions = ((1, has_ahead, ahead), (-1, has_behind, behind))

    def at_distance(step, run):
        for way, onward, target in directions:
            far = z - way * step
            pl.when((far >= 0) & (far < line))(functools.partial(run, far, onward, target))

    def along(step, act, wait):
        def run(far, onward, target):
            source = index(far, lane, core)
            for piece in (1, 2):
                if wait:
                    arrived(source, piece)
                pl.when(onward)(lambda: act(relay_copies(source, piece, 0, target)))
                act(relay_copies(source, piece, 1, across))
                act(relay_copies(source, piece, 2, partner))
        at_distance(step, run)

    def along_short(step, act, wait):
        def run(far, onward, target):
            for yy in (lane, 1 - lane):
                source = index(far, yy, core)
                if wait:
                    arrived(source, 0)
                pl.when(onward)(lambda: act(relay_copies(source, 0, 0, target)))
                act(relay_copies(source, 0, 2, partner))
        at_distance(step, run)

    def crossed(source, act, wait):
        for piece in (1, 2):
            if wait:
                arrived(source, piece)
            act(relay_copies(source, piece, 2, partner))

    def crossed_short(act, wait):
        if wait:
            arrived(across, 0)
        pl.when(has_ahead)(lambda: act(relay_copies(across, 0, 0, ahead)))
        pl.when(has_behind)(lambda: act(relay_copies(across, 0, 1, behind)))
        act(relay_copies(across, 0, 2, partner))

    def crossed_far(step, act, wait):
        at_distance(step, lambda far, onward, target: crossed(index(far, 1 - lane, core), act, wait))

    def attend(keys_of, values_of, key_pos):
        low = low_ref[...]
        high = high_ref[...]
        within = lax.broadcasted_iota(jnp.int32, (1, group), 1)
        bias = []
        for g in range(2):
            here = key_pos(g) * group + within
            bias.append(jnp.where((here >= low) & (here <= high), 0.0, -1e30))
        bias = jnp.concatenate(bias, axis=1)
        for h in range(heads):
            column = pl.ds(h * HEAD_DIM, HEAD_DIM)
            scores = lax.dot_general(
                q_ref[:, column], keys_of(h), (((1,), (1,)), ((), ())), preferred_element_type=jnp.float32
            ) + bias
            before = top[h]
            now = jnp.maximum(before, jnp.max(scores, axis=1, keepdims=True))
            weights = jnp.exp2((scores - jnp.concatenate([now] * (rows // HEAD_DIM), axis=1)) * factor)
            fade = jnp.exp2((before - now) * factor)
            top[h] = now
            total[h] = total[h] * fade + jnp.sum(weights, axis=1, keepdims=True)
            acc[:, column] = acc[:, column] * fade + jnp.dot(
                weights.astype(jnp.bfloat16), values_of(h), preferred_element_type=jnp.float32
            )

    def attend_stored(source):
        attend(
            lambda h: kv[source, :, pl.ds(h * HEAD_DIM, HEAD_DIM)],
            lambda h: kv[source, :, pl.ds(cols + h * HEAD_DIM, HEAD_DIM)],
            lambda g: posb[source][:, g:g + 1],
        )

    def attend_second(source):
        for piece in range(3):
            arrived(source, piece)
        attend_stored(source)

    def attend_far(step):
        def run(far, onward, target):
            def one(j, carry):
                yy = lax.rem(lane + j, 2)
                attend_stored(index(far, yy, core))
                attend_second(index(far, yy, 1 - core))
                return carry
            lax.fori_loop(0, 2, one, 0)
        at_distance(step, run)

    for one in loads:
        one.wait()
    own_routes(start_all)
    top[...] = jnp.full_like(top, -1e30)
    total[...] = jnp.zeros_like(total)
    acc[...] = jnp.zeros_like(acc)
    down = lax.broadcasted_iota(jnp.int32, (group, group), 0)
    right = lax.broadcasted_iota(jnp.int32, (group, group), 1)
    for g in range(2):
        own_group = table_ref[0, g]
        own_doc = jnp.broadcast_to(doc_ref[pl.ds(own_group, 1), :], (group, group))
        own_doc = jnp.sum(jnp.where(down == right, own_doc, 0), axis=1, keepdims=True)

        def count(i, found):
            return found + (doc_ref[pl.ds(i, 1), :] < own_doc).astype(jnp.int32)

        found = lax.fori_loop(0, doc_ref.shape[0], count, jnp.zeros((group, group), jnp.int32))
        part = pl.ds(g * group, group)
        low_ref[part, :] = jnp.broadcast_to(jnp.sum(found, axis=1, keepdims=True), (group, group))
        high_ref[part, :] = own_group * group + down
    attend_stored(me)
    crossed_short(start_all, True)
    attend_second(partner)

    along(1, start_all, True)
    crossed(across, start_all, True)
    along_short(1, start_all, True)
    attend_stored(across)
    attend_second(index(z, 1 - lane, 1 - core))

    def loop(step, carry):
        along(step, start_all, True)
        along_short(step, start_all, True)
        crossed_far(step - 1, start_all, True)
        attend_far(step - 1)
        return carry

    lax.fori_loop(2, line + 1, loop, 0)

    for h in range(heads):
        column = pl.ds(h * HEAD_DIM, HEAD_DIM)
        out_ref[:, column] = (acc[:, column] / total[h]).astype(out_ref.dtype)

    own_routes(end_sends)
    crossed_short(end_sends, False)
    crossed(across, end_sends, False)

    def drain(step, carry):
        along(step, end_sends, False)
        along_short(step, end_sends, False)
        crossed_far(step, end_sends, False)
        return carry

    lax.fori_loop(1, line, drain, 0)


def solution(mesh):
    members = mesh.shape["blk"]
    line = members // (CORES * LANES)

    def shards(queries, keys, values, group_table, doc_ids):
        rows, cols = queries.shape
        group = rows // 2
        heads = cols // HEAD_DIM
        doc_rows = doc_ids.reshape(-1, group)
        vmem = pl.BlockSpec(memory_space=pltpu.VMEM)
        return pl.pallas_call(
            functools.partial(attend_kernel, line),
            out_shape=jax.ShapeDtypeStruct((rows, cols), jnp.bfloat16),
            in_specs=[pl.BlockSpec(memory_space=pltpu.SMEM)] + [pl.BlockSpec(memory_space=pl.ANY)] * 4 + [vmem],
            out_specs=vmem,
            scratch_shapes=[
                pltpu.VMEM((members, rows, 2 * cols), jnp.bfloat16),
                pltpu.VMEM((members, 1, 2), jnp.int32),
                pltpu.VMEM((rows, cols), jnp.bfloat16),
                pltpu.VMEM((rows, group), jnp.int32),
                pltpu.VMEM((rows, group), jnp.int32),
                pltpu.VMEM((heads, rows, HEAD_DIM), jnp.float32),
                pltpu.VMEM((heads, rows, HEAD_DIM), jnp.float32),
                pltpu.VMEM((rows, cols), jnp.float32),
                pltpu.SemaphoreType.DMA((members, 3)),
                pltpu.SemaphoreType.DMA((members,)),
                pltpu.SemaphoreType.DMA((members, 3, 4)),
                pltpu.SemaphoreType.DMA((members, 4)),
                pltpu.SemaphoreType.DMA((4,)),
            ],
            compiler_params=pltpu.CompilerParams(
                collective_id=0, has_side_effects=True, vmem_limit_bytes=60 * 1024 * 1024
            ),
        )(group_table, queries, keys, values, group_table, doc_rows)

    in_specs = (P("blk", "head"), P("blk", "head"), P("blk", "head"), P("blk", None), P())
    return jax.shard_map(shards, mesh=mesh, in_specs=in_specs, out_specs=P("blk", "head"), check_vma=False)
```

profile of v0, /device:TPU:0, one launch (start us, length us, event | category | flops | bytes accessed | tf_op | source)
XLA Modules:
  0.0 56.4 jit_solution(910981080922516753)
XLA Ops:
  0.0 54.8 %shard_map.55 = bf16[256,512]{1,0:T(8,128)(2,1)} custom-call(s32[1,2]{1,0:T(1,128)} %table_hbm.1, bf16[256,512]{1,0:T(8,128)(2,1)} %q_hbm.1, bf16[256,512]{1,0:T(8,128)(2,1)} %k_hbm.1, bf16[256,512]{1,0:T(8,128)(2,1)} %v_hbm.1, s32[1,2]{1,0:T(1,128)} %table_hbm.1, s32[32,128]{1,0:T(8,128)} %bitcast.1), custom_call_target="tpu_custom_call" | custom-call | tf_op jit(solution)/shard_map/pallas_call | solution.py:251
  54.8 1.7 %copy.7 = bf16[256,512]{1,0:T(8,128)(2,1)} copy(bf16[256,512]{1,0:T(8,128)(2,1)} %shard_map.55) | data formatting | bytes 524288
where the time goes:
time: 56.7 us; the launch traced here: 56.4 us
  Pallas kernels  54.8 us (97%)
  local copies, waits for them, and re-layouts  1.67 us (3%)
    pallas_call x1, Pallas kernels, shards(): pl.pallas_call(functools.partial(attend_kernel, line), out_shape=jax.Shap...  54.8 us
    unnamed x1, local copies, waits for them, and re-layouts  1.67 us

commit v1 on v0

v1 whole, which is shorter than its diff:
```python
import functools
import math

import jax
import jax.numpy as jnp
from jax import lax
from jax.experimental import pallas as pl
from jax.experimental.pallas import tpu as pltpu
from jax.sharding import PartitionSpec as P

HEAD_DIM = 128
CORES = 2
MASKED = -1e30


def attend_kernel(
    cells, table_ref, q_hbm, k_hbm, v_hbm, doc_ref, out_ref,
    stage_q, stage_kv, qin, kv, meta, osend, ssend, obuf, sbuf,
    load_q, load_kv, own_sem, q_send, q_recv, kv_send, kv_recv, fwd_send, m_send, m_recv, mf_send,
    o_send, o_recv, s_send, s_recv,
):
    rows, cols = q_hbm.shape
    heads = cols // HEAD_DIM
    group = rows // 2
    factor = math.log2(math.e) / math.sqrt(HEAD_DIM)
    me = lax.axis_index("blk")
    core = lax.rem(me, CORES)
    chip = lax.rem(me // CORES, heads)
    cell = me // (CORES * heads)

    def index(cc, ch, co):
        return (cc * heads + ch) * CORES + co

    partner = index(cell, chip, 1 - core)

    def head_columns(h):
        start = h * HEAD_DIM
        if not isinstance(h, int):
            start = pl.multiple_of(start, HEAD_DIM)
        return pl.ds(start, HEAD_DIM)

    def own_slot(ch, co):
        return ch * CORES + co

    q_loads = [pltpu.make_async_copy(q_hbm.at[:, head_columns(h)], stage_q.at[h], load_q.at[h]) for h in range(heads)]
    kv_loads = []
    for h in range(heads):
        kv_loads.append((
            pltpu.make_async_copy(k_hbm.at[:, head_columns(h)], stage_kv.at[h, :, pl.ds(0, HEAD_DIM)], load_kv.at[h, 0]),
            pltpu.make_async_copy(v_hbm.at[:, head_columns(h)], stage_kv.at[h, :, pl.ds(HEAD_DIM, HEAD_DIM)], load_kv.at[h, 1]),
        ))
    own_kv = (
        pltpu.make_async_copy(k_hbm.at[:, head_columns(chip)], kv.at[own_slot(chip, core), :, pl.ds(0, HEAD_DIM)], own_sem.at[0]),
        pltpu.make_async_copy(v_hbm.at[:, head_columns(chip)], kv.at[own_slot(chip, core), :, pl.ds(HEAD_DIM, HEAD_DIM)], own_sem.at[1]),
    )
    own_q = pltpu.make_async_copy(q_hbm.at[:, head_columns(chip)], qin.at[cell, chip], own_sem.at[2])
    for one in q_loads:
        one.start()
    for pair in kv_loads:
        for one in pair:
            one.start()
    for one in own_kv:
        one.start()
    own_q.start()

    barrier = pltpu.get_barrier_semaphore()
    peers = []
    for k in range(cells):
        for i in range(heads):
            if k or i:
                peers.append((lax.rem(cell + k, cells), lax.rem(chip + i, heads), k * heads + i))
    for cc, ch, _ in peers:
        pl.semaphore_signal(barrier, inc=1, device_id={"blk": index(cc, ch, core)})
    pl.semaphore_signal(barrier, inc=1, device_id={"blk": partner})

    within = lax.broadcasted_iota(jnp.int32, (1, group), 1)
    for g in range(2):
        own_group = table_ref[0, g]
        meta[me, pl.ds(g, 1), :] = doc_ref[pl.ds(own_group, 1), :]
        meta[me, pl.ds(2 + g, 1), :] = own_group * group + within

    pl.semaphore_wait(barrier, len(peers) + 1)

    def remote(src, dst, ssem, rsem, target):
        return pltpu.make_async_remote_copy(
            src_ref=src, dst_ref=dst, send_sem=ssem, recv_sem=rsem, device_id={"blk": target}
        )

    def q_copy(cc, ch, n):
        return remote(stage_q.at[ch], qin.at[cell, chip], q_send.at[n], q_recv.at[cell, chip], index(cc, ch, core))

    def kv_copy(ch, n):
        place = own_slot(chip, core)
        return remote(stage_kv.at[ch], kv.at[place], kv_send.at[n], kv_recv.at[place], index(cell, ch, core))

    def kv_forward(ch):
        place = own_slot(ch, core)
        return remote(kv.at[place], kv.at[place], fwd_send.at[ch], kv_recv.at[place], partner)

    def meta_copy(cc, ch, n):
        return remote(meta.at[me], meta.at[me], m_send.at[n], m_recv.at[me], index(cc, ch, core))

    def meta_forward(ch):
        source = index(cell, ch, core)
        return remote(meta.at[source], meta.at[source], mf_send.at[ch], m_recv.at[source], partner)

    def q_arrival(cc, ch):
        return remote(stage_q.at[0], qin.at[cc, ch], q_send.at[0], q_recv.at[cc, ch], partner)

    def kv_arrival(place):
        return remote(kv.at[place], kv.at[place], fwd_send.at[0], kv_recv.at[place], partner)

    def meta_arrival(source):
        return remote(meta.at[source], meta.at[source], mf_send.at[0], m_recv.at[source], partner)

    near = [one for one in peers if one[2] < heads]
    far = [one for one in peers if one[2] >= heads]
    for one in q_loads:
        one.wait()
    for cc, ch, n in near:
        q_copy(cc, ch, n).start()
    for pair in kv_loads:
        for one in pair:
            one.wait()
    for cc, ch, n in near:
        kv_copy(ch, n).start()
    for cc, ch, n in near:
        meta_copy(cc, ch, n).start()
    for cc, ch, n in far:
        q_copy(cc, ch, n).start()
    for cc, ch, n in far:
        meta_copy(cc, ch, n).start()
    for one in own_kv:
        one.wait()
    kv_forward(chip).start()
    meta_forward(chip).start()
    own_q.wait()
    for cc, ch, n in near:
        kv_arrival(own_slot(ch, core)).wait_recv()
        kv_forward(ch).start()
        meta_arrival(index(cell, ch, core)).wait_recv()
        meta_forward(ch).start()
    for i in range(heads):
        ch = lax.rem(chip + i, heads)
        kv_arrival(own_slot(ch, 1 - core)).wait_recv()
        meta_arrival(index(cell, ch, 1 - core)).wait_recv()

    sources = heads * CORES
    key_doc = [[meta[cell * sources + s, pl.ds(g, 1), :] for s in range(sources)] for g in range(2)]
    key_pos = [[meta[cell * sources + s, pl.ds(2 + g, 1), :] for s in range(sources)] for g in range(2)]
    down = lax.broadcasted_iota(jnp.int32, (group, group), 0)
    right = lax.broadcasted_iota(jnp.int32, (group, group), 1)
    diagonal = down == right

    def to_rows(line):
        return jnp.sum(jnp.where(diagonal, line, 0), axis=1, keepdims=True)

    def to_lanes(column):
        return jnp.sum(jnp.where(diagonal, column, 0), axis=0, keepdims=True)

    def attend(q, source, slot):
        doc = jnp.broadcast_to(to_rows(meta[source, pl.ds(slot, 1), :]), (group, group))
        pos = jnp.broadcast_to(to_rows(meta[source, pl.ds(2 + slot, 1), :]), (group, group))
        parts = []
        for g in range(slot + 1):
            keys = kv[:, pl.ds(g * group, group), pl.ds(0, HEAD_DIM)].reshape(sources * group, HEAD_DIM)
            scores = lax.dot_general(q, keys, (((1,), (1,)), ((), ())), preferred_element_type=jnp.float32)
            for s in range(sources):
                seen = (key_doc[g][s] == doc) & (key_pos[g][s] <= pos)
                parts.append(jnp.where(seen, scores[:, s * group:(s + 1) * group], MASKED))
        best = parts[0]
        for one in parts[1:]:
            best = jnp.maximum(best, one)
        best = jnp.broadcast_to(jnp.max(best, axis=1, keepdims=True), (group, group))
        total = None
        out = None
        for g in range(slot + 1):
            weights = [jnp.exp2((one - best) * factor) for one in parts[g * sources:(g + 1) * sources]]
            for one in weights:
                total = one if total is None else total + one
            weights = jnp.concatenate([one.astype(jnp.bfloat16) for one in weights], axis=1)
            vals = kv[:, pl.ds(g * group, group), pl.ds(HEAD_DIM, HEAD_DIM)].reshape(sources * group, HEAD_DIM)
            add = jnp.dot(weights, vals, preferred_element_type=jnp.float32)
            out = add if out is None else out + add
        total = jnp.broadcast_to(jnp.sum(total, axis=1, keepdims=True), (group, group))
        return out, to_lanes(best), to_lanes(total)

    def o_copy(cc, ch, n):
        return remote(osend.at[n], obuf.at[cell, chip], o_send.at[n], o_recv.at[cell, chip], index(cc, ch, core))

    def s_copy(cc, ch, n):
        return remote(ssend.at[n], sbuf.at[cell, chip], s_send.at[n], s_recv.at[cell, chip], index(cc, ch, core))

    def o_arrival(cc, h):
        return remote(osend.at[0], obuf.at[cc, h], o_send.at[0], o_recv.at[cc, h], partner)

    def s_arrival(cc, h):
        return remote(ssend.at[0], sbuf.at[cc, h], s_send.at[0], s_recv.at[cc, h], partner)

    def place_of(t):
        return lax.rem(cell + 1 + t // heads, cells), lax.rem(chip + lax.rem(t, heads), heads)

    def serve(t, carry):
        cc, ch = place_of(t)
        home = index(cc, ch, core)
        other = home != me

        def arrive():
            q_arrival(cc, ch).wait_recv()

        pl.when(other)(arrive)

        def arrive_meta():
            meta_arrival(home).wait_recv()

        pl.when(cc != cell)(arrive_meta)
        for slot in range(2):
            q = qin[cc, ch, pl.ds(slot * group, group), :]
            out, best, total = attend(q, home, slot)
            osend[t, pl.ds(slot * group, group), :] = out.astype(jnp.bfloat16)
            ssend[t, pl.ds(slot, 1), :] = best
            ssend[t, pl.ds(2 + slot, 1), :] = total

        def give():
            o_copy(cc, ch, t).start()
            s_copy(cc, ch, t).start()

        pl.when(other)(give)
        return carry

    lax.fori_loop(0, cells * heads, serve, 0)

    own_turn = (cells - 1) * heads
    obuf[cell, chip] = osend[own_turn]
    sbuf[cell, chip] = ssend[own_turn]

    for h in range(heads):
        column = pl.ds(h * HEAD_DIM, HEAD_DIM)
        for cc in range(cells):
            def arrive_partial():
                o_arrival(cc, h).wait_recv()
                s_arrival(cc, h).wait_recv()

            pl.when((cell != cc) | (chip != h))(arrive_partial)
        for slot in range(2):
            part = pl.ds(slot * group, group)
            tops = [sbuf[cc, h, pl.ds(slot, 1), :] for cc in range(cells)]
            sums = [sbuf[cc, h, pl.ds(2 + slot, 1), :] for cc in range(cells)]
            top = functools.reduce(jnp.maximum, tops)
            scale = [jnp.exp2((one - top) * factor) for one in tops]
            total = functools.reduce(jnp.add, [a * b for a, b in zip(scale, sums)])
            mixed = None
            for cc in range(cells):
                weight = to_rows(scale[cc] / total)
                term = obuf[cc, h, part, :].astype(jnp.float32) * weight
                mixed = term if mixed is None else mixed + term
            out_ref[part, column] = mixed.astype(out_ref.dtype)

    for cc, ch, n in peers:
        q_copy(cc, ch, n).wait_send()
        meta_copy(cc, ch, n).wait_send()
    for cc, ch, n in near:
        kv_copy(ch, n).wait_send()
    for ch in range(heads):
        kv_forward(ch).wait_send()
        meta_forward(ch).wait_send()

    def drain(t, carry):
        cc, ch = place_of(t)

        def finish():
            o_copy(cc, ch, t).wait_send()
            s_copy(cc, ch, t).wait_send()

        pl.when(index(cc, ch, core) != me)(finish)
        return carry

    lax.fori_loop(0, cells * heads, drain, 0)


def solution(mesh):
    members = mesh.shape["blk"]

    def shards(queries, keys, values, group_table, doc_ids):
        rows, cols = queries.shape
        group = rows // 2
        heads = cols // HEAD_DIM
        cells = members // (heads * CORES)
        doc_rows = doc_ids.reshape(-1, group)
        vmem = pl.BlockSpec(memory_space=pltpu.VMEM)
        bf16, f32 = jnp.bfloat16, jnp.float32
        dma = pltpu.SemaphoreType.DMA
        return pl.pallas_call(
            functools.partial(attend_kernel, cells),
            out_shape=jax.ShapeDtypeStruct((rows, cols), bf16),
            in_specs=[pl.BlockSpec(memory_space=pltpu.SMEM)] + [pl.BlockSpec(memory_space=pl.ANY)] * 3 + [vmem],
            out_specs=vmem,
            scratch_shapes=[
                pltpu.VMEM((heads, rows, HEAD_DIM), bf16),
                pltpu.VMEM((heads, rows, 2 * HEAD_DIM), bf16),
                pltpu.VMEM((cells, heads, rows, HEAD_DIM), bf16),
                pltpu.VMEM((heads * CORES, rows, 2 * HEAD_DIM), bf16),
                pltpu.VMEM((members, 4, group), jnp.int32),
                pltpu.VMEM((cells * heads, rows, HEAD_DIM), bf16),
                pltpu.VMEM((cells * heads, 4, group), f32),
                pltpu.VMEM((cells, heads, rows, HEAD_DIM), bf16),
                pltpu.VMEM((cells, heads, 4, group), f32),
                dma((heads,)),
                dma((heads, 2)),
                dma((3,)),
                dma((cells * heads,)),
                dma((cells, heads)),
                dma((heads,)),
                dma((heads * CORES,)),
                dma((heads,)),
                dma((cells * heads,)),
                dma((members,)),
                dma((heads,)),
                dma((cells * heads,)),
                dma((cells, heads)),
                dma((cells * heads,)),
                dma((cells, heads)),
            ],
            compiler_params=pltpu.CompilerParams(
                collective_id=0, has_side_effects=True, vmem_limit_bytes=60 * 1024 * 1024
            ),
        )(group_table, queries, keys, values, doc_rows)

    in_specs = (P("blk", "head"), P("blk", "head"), P("blk", "head"), P("blk", None), P())
    return jax.shard_map(shards, mesh=mesh, in_specs=in_specs, out_specs=P("blk", "head"), check_vma=False)
```

time: 56.7 us -> 40.5 us (0.71)
  Pallas kernels: 54.8 us -> 38.6 us
    pallas_call x1, Pallas kernels: 54.8 us -> 38.6 us  [shards(): pl.pallas_call(functools.partial(attend_kernel, cells), out_shape=jax.Sha...]
where the time goes in v1:
time: 40.5 us; the launch traced here: 40.2 us
  Pallas kernels  38.6 us (95%)
  local copies, waits for them, and re-layouts  1.67 us (4%)
    pallas_call x1, Pallas kernels, shards(): pl.pallas_call(functools.partial(attend_kernel, cells), out_shape=jax.Sha...  38.6 us
    unnamed x1, local copies, waits for them, and re-layouts  1.67 us

profile of v1, /device:TPU:0, one launch (start us, length us, event | category | flops | bytes accessed | tf_op | source)
XLA Modules:
  0.0 40.2 jit_solution(2012039182760578345)
XLA Ops:
  0.0 38.6 %shard_map.55 = bf16[256,512]{1,0:T(8,128)(2,1)} custom-call(s32[1,2]{1,0:T(1,128)} %table_ref.1, bf16[256,512]{1,0:T(8,128)(2,1)} %q_hbm.1, bf16[256,512]{1,0:T(8,128)(2,1)} %k_hbm.1, bf16[256,512]{1,0:T(8,128)(2,1)} %v_hbm.1, s32[32,128]{1,0:T(8,128)} %bitcast.1), custom_call_target="tpu_custom_call" | custom-call | tf_op jit(solution)/shard_map/pallas_call | solution.py:293
  38.6 1.7 %copy.7 = bf16[256,512]{1,0:T(8,128)(2,1)} copy(bf16[256,512]{1,0:T(8,128)(2,1)} %shard_map.55) | data formatting | bytes 524288

commit v2 on v1

--- a/solution.py
+++ b/solution.py
@@ -14,9 +14,9 @@
 
 
 def attend_kernel(
-    cells, table_ref, q_hbm, k_hbm, v_hbm, doc_ref, out_ref,
-    stage_q, stage_kv, qin, kv, meta, osend, ssend, obuf, sbuf,
-    load_q, load_kv, own_sem, q_send, q_recv, kv_send, kv_recv, fwd_send, m_send, m_recv, mf_send,
+    cells, table_hbm, q_hbm, k_hbm, v_hbm, doc_hbm, out_hbm,
+    table_ref, doc_ref, mixed_ref, stage_q, stage_kv, qin, kv, meta, osend, ssend, obuf, sbuf,
+    small_sem, out_sem, load_q, load_kv, own_sem, q_send, q_recv, kv_send, kv_recv, fwd_send, m_send, m_recv, mf_send,
     o_send, o_recv, s_send, s_recv,
 ):
     rows, cols = q_hbm.shape
@@ -54,12 +54,18 @@
         pltpu.make_async_copy(v_hbm.at[:, head_columns(chip)], kv.at[own_slot(chip, core), :, pl.ds(HEAD_DIM, HEAD_DIM)], own_sem.at[1]),
     )
     own_q = pltpu.make_async_copy(q_hbm.at[:, head_columns(chip)], qin.at[cell, chip], own_sem.at[2])
-    for one in q_loads:
+    small_loads = (
+        pltpu.make_async_copy(table_hbm, table_ref, small_sem.at[0]),
+        pltpu.make_async_copy(doc_hbm, doc_ref, small_sem.at[1]),
+    )
+    for one in small_loads:
         one.start()
     for pair in kv_loads:
         for one in pair:
             one.start()
     for one in own_kv:
+        one.start()
+    for one in q_loads:
         one.start()
     own_q.start()
 
@@ -73,12 +79,13 @@
         pl.semaphore_signal(barrier, inc=1, device_id={"blk": index(cc, ch, core)})
     pl.semaphore_signal(barrier, inc=1, device_id={"blk": partner})
 
+    for one in small_loads:
+        one.wait()
     within = lax.broadcasted_iota(jnp.int32, (1, group), 1)
     for g in range(2):
         own_group = table_ref[0, g]
         meta[me, pl.ds(g, 1), :] = doc_ref[pl.ds(own_group, 1), :]
         meta[me, pl.ds(2 + g, 1), :] = own_group * group + within
-
     pl.semaphore_wait(barrier, len(peers) + 1)
 
     def remote(src, dst, ssem, rsem, target):
@@ -115,25 +122,23 @@
 
     near = [one for one in peers if one[2] < heads]
     far = [one for one in peers if one[2] >= heads]
-    for one in q_loads:
-        one.wait()
-    for cc, ch, n in near:
-        q_copy(cc, ch, n).start()
     for pair in kv_loads:
         for one in pair:
             one.wait()
     for cc, ch, n in near:
         kv_copy(ch, n).start()
-    for cc, ch, n in near:
+    for cc, ch, n in peers:
         meta_copy(cc, ch, n).start()
-    for cc, ch, n in far:
-        q_copy(cc, ch, n).start()
-    for cc, ch, n in far:
-        meta_copy(cc, ch, n).start()
+    meta_forward(chip).start()
     for one in own_kv:
         one.wait()
     kv_forward(chip).start()
-    meta_forward(chip).start()
+    for one in q_loads:
+        one.wait()
+    for cc, ch, n in far:
+        q_copy(cc, ch, n).start()
+    for cc, ch, n in near:
+        q_copy(cc, ch, n).start()
     own_q.wait()
     for cc, ch, n in near:
         kv_arrival(own_slot(ch, core)).wait_recv()
@@ -234,8 +239,10 @@
     obuf[cell, chip] = osend[own_turn]
     sbuf[cell, chip] = ssend[own_turn]
 
+    def out_copy(h):
+        return pltpu.make_async_copy(mixed_ref.at[h], out_hbm.at[:, head_columns(h)], out_sem.at[h])
+
     for h in range(heads):
-        column = pl.ds(h * HEAD_DIM, HEAD_DIM)
         for cc in range(cells):
             def arrive_partial():
                 o_arrival(cc, h).wait_recv()
@@ -254,7 +261,8 @@
                 weight = to_rows(scale[cc] / total)
                 term = obuf[cc, h, part, :].astype(jnp.float32) * weight
                 mixed = term if mixed is None else mixed + term
-            out_ref[part, column] = mixed.astype(out_ref.dtype)
+            mixed_ref[h, part, :] = mixed.astype(mixed_ref.dtype)
+        out_copy(h).start()
 
     for cc, ch, n in peers:
         q_copy(cc, ch, n).wait_send()
@@ -276,6 +284,8 @@
         return carry
 
     lax.fori_loop(0, cells * heads, drain, 0)
+    for h in range(heads):
+        out_copy(h).wait()
 
 
 def solution(mesh):
@@ -287,15 +297,17 @@
         heads = cols // HEAD_DIM
         cells = members // (heads * CORES)
         doc_rows = doc_ids.reshape(-1, group)
-        vmem = pl.BlockSpec(memory_space=pltpu.VMEM)
         bf16, f32 = jnp.bfloat16, jnp.float32
         dma = pltpu.SemaphoreType.DMA
         return pl.pallas_call(
             functools.partial(attend_kernel, cells),
             out_shape=jax.ShapeDtypeStruct((rows, cols), bf16),
-            in_specs=[pl.BlockSpec(memory_space=pltpu.SMEM)] + [pl.BlockSpec(memory_space=pl.ANY)] * 3 + [vmem],
-            out_specs=vmem,
+            in_specs=[pl.BlockSpec(memory_space=pl.ANY)] * 5,
+            out_specs=pl.BlockSpec(memory_space=pl.ANY),
             scratch_shapes=[
+                pltpu.SMEM((1, 2), jnp.int32),
+                pltpu.VMEM(doc_rows.shape, jnp.int32),
+                pltpu.VMEM((heads, rows, HEAD_DIM), bf16),
                 pltpu.VMEM((heads, rows, HEAD_DIM), bf16),
                 pltpu.VMEM((heads, rows, 2 * HEAD_DIM), bf16),
                 pltpu.VMEM((cells, heads, rows, HEAD_DIM), bf16),
@@ -305,6 +317,8 @@
                 pltpu.VMEM((cells * heads, 4, group), f32),
                 pltpu.VMEM((cells, heads, rows, HEAD_DIM), bf16),
                 pltpu.VMEM((cells, heads, 4, group), f32),
+                dma((2,)),
+                dma((heads,)),
                 dma((heads,)),
                 dma((heads, 2)),
                 dma((3,)),

time: 40.5 us -> 36.9 us (0.911)
  Pallas kernels: 38.6 us -> 35 us
    pallas_call x1, Pallas kernels: 38.6 us -> 35 us  [shards(): pl.pallas_call(functools.partial(attend_kernel, cells), out_shape=jax.Sha...]
where the time goes in v2:
time: 36.9 us; the launch traced here: 36.7 us
  Pallas kernels  35 us (95%)
  local copies, waits for them, and re-layouts  1.67 us (5%)
    pallas_call x1, Pallas kernels, shards(): pl.pallas_call(functools.partial(attend_kernel, cells), out_shape=jax.Sha...  35 us
    unnamed x1, local copies, waits for them, and re-layouts  1.67 us

profile of v2, /device:TPU:0, one launch (start us, length us, event | category | flops | bytes accessed | tf_op | source)
XLA Modules:
  0.0 36.7 jit_solution(7851413006966372625)
XLA Ops:
  0.0 35.0 %shard_map.55 = bf16[256,512]{1,0:T(8,128)(2,1)} custom-call(s32[1,2]{1,0:T(1,128)} %table_hbm.1, bf16[256,512]{1,0:T(8,128)(2,1)} %q_hbm.1, bf16[256,512]{1,0:T(8,128)(2,1)} %k_hbm.1, bf16[256,512]{1,0:T(8,128)(2,1)} %v_hbm.1, s32[32,128]{1,0:T(8,128)} %bitcast.1), custom_call_target="tpu_custom_call" | custom-call | tf_op jit(solution)/shard_map/pallas_call | solution.py:302
  35.0 1.7 %copy.7 = bf16[256,512]{1,0:T(8,128)(2,1)} copy(bf16[256,512]{1,0:T(8,128)(2,1)} %shard_map.55) | data formatting | bytes 524288

commit v3 on v2

--- a/solution.py
+++ b/solution.py
@@ -32,6 +32,9 @@
         return (cc * heads + ch) * CORES + co
 
     partner = index(cell, chip, 1 - core)
+
+    def facing(other, i):
+        return lax.rem(i + (heads // 2) * (other < cell).astype(jnp.int32), heads)
 
     def head_columns(h):
         start = h * HEAD_DIM
@@ -71,10 +74,12 @@
 
     barrier = pltpu.get_barrier_semaphore()
     peers = []
-    for k in range(cells):
+    for i in range(heads - 1, 0, -1):
+        peers.append((cell, chip ^ i, i))
+    for k in range(1, cells):
+        other = lax.rem(cell + k, cells)
         for i in range(heads):
-            if k or i:
-                peers.append((lax.rem(cell + k, cells), lax.rem(chip + i, heads), k * heads + i))
+            peers.append((other, facing(other, i) ^ lax.rem(chip, 2), k * heads + i))
     for cc, ch, _ in peers:
         pl.semaphore_signal(barrier, inc=1, device_id={"blk": index(cc, ch, core)})
     pl.semaphore_signal(barrier, inc=1, device_id={"blk": partner})
@@ -84,8 +89,8 @@
     within = lax.broadcasted_iota(jnp.int32, (1, group), 1)
     for g in range(2):
         own_group = table_ref[0, g]
-        meta[me, pl.ds(g, 1), :] = doc_ref[pl.ds(own_group, 1), :]
-        meta[me, pl.ds(2 + g, 1), :] = own_group * group + within
+        meta[me, pl.ds(g, 1), :] = doc_ref[pl.ds(own_group, 1), :].astype(jnp.float32)
+        meta[me, pl.ds(2 + g, 1), :] = (own_group * group + within).astype(jnp.float32)
     pl.semaphore_wait(barrier, len(peers) + 1)
 
     def remote(src, dst, ssem, rsem, target):
@@ -122,14 +127,14 @@
 
     near = [one for one in peers if one[2] < heads]
     far = [one for one in peers if one[2] >= heads]
+    for cc, ch, n in peers:
+        meta_copy(cc, ch, n).start()
+    meta_forward(chip).start()
     for pair in kv_loads:
         for one in pair:
             one.wait()
     for cc, ch, n in near:
         kv_copy(ch, n).start()
-    for cc, ch, n in peers:
-        meta_copy(cc, ch, n).start()
-    meta_forward(chip).start()
     for one in own_kv:
         one.wait()
     kv_forward(chip).start()
@@ -151,44 +156,60 @@
         meta_arrival(index(cell, ch, 1 - core)).wait_recv()
 
     sources = heads * CORES
-    key_doc = [[meta[cell * sources + s, pl.ds(g, 1), :] for s in range(sources)] for g in range(2)]
-    key_pos = [[meta[cell * sources + s, pl.ds(2 + g, 1), :] for s in range(sources)] for g in range(2)]
     down = lax.broadcasted_iota(jnp.int32, (group, group), 0)
     right = lax.broadcasted_iota(jnp.int32, (group, group), 1)
     diagonal = down == right
 
     def to_rows(line):
-        return jnp.sum(jnp.where(diagonal, line, 0), axis=1, keepdims=True)
+        return jnp.sum(jnp.where(diagonal, line, 0.0), axis=1, keepdims=True)
 
     def to_lanes(column):
-        return jnp.sum(jnp.where(diagonal, column, 0), axis=0, keepdims=True)
-
-    def attend(q, source, slot):
-        doc = jnp.broadcast_to(to_rows(meta[source, pl.ds(slot, 1), :]), (group, group))
-        pos = jnp.broadcast_to(to_rows(meta[source, pl.ds(2 + slot, 1), :]), (group, group))
-        parts = []
-        for g in range(slot + 1):
-            keys = kv[:, pl.ds(g * group, group), pl.ds(0, HEAD_DIM)].reshape(sources * group, HEAD_DIM)
-            scores = lax.dot_general(q, keys, (((1,), (1,)), ((), ())), preferred_element_type=jnp.float32)
-            for s in range(sources):
-                seen = (key_doc[g][s] == doc) & (key_pos[g][s] <= pos)
-                parts.append(jnp.where(seen, scores[:, s * group:(s + 1) * group], MASKED))
-        best = parts[0]
-        for one in parts[1:]:
-            best = jnp.maximum(best, one)
-        best = jnp.broadcast_to(jnp.max(best, axis=1, keepdims=True), (group, group))
-        total = None
-        out = None
-        for g in range(slot + 1):
-            weights = [jnp.exp2((one - best) * factor) for one in parts[g * sources:(g + 1) * sources]]
-            for one in weights:
-                total = one if total is None else total + one
-            weights = jnp.concatenate([one.astype(jnp.bfloat16) for one in weights], axis=1)
-            vals = kv[:, pl.ds(g * group, group), pl.ds(HEAD_DIM, HEAD_DIM)].reshape(sources * group, HEAD_DIM)
-            add = jnp.dot(weights, vals, preferred_element_type=jnp.float32)
-            out = add if out is None else out + add
-        total = jnp.broadcast_to(jnp.sum(total, axis=1, keepdims=True), (group, group))
-        return out, to_lanes(best), to_lanes(total)
+        return jnp.sum(jnp.where(diagonal, column, 0.0), axis=0, keepdims=True)
+
+    def attend(cc, ch, home):
+        order = [lax.rem(own_slot(ch, core) + i, sources) for i in range(sources)]
+        q = qin[cc, ch]
+        doc_line = [meta[home, pl.ds(slot, 1), :] for slot in range(2)]
+        pos_line = [meta[home, pl.ds(2 + slot, 1), :] for slot in range(2)]
+        doc = [jnp.broadcast_to(to_rows(one), (group, group)) for one in doc_line]
+        pos = [jnp.broadcast_to(to_rows(one), (group, group)) for one in pos_line]
+        parts = [[], []]
+        for g in range(2):
+            part = pl.ds(g * group, group)
+            keys = jnp.concatenate([kv[s, part, pl.ds(0, HEAD_DIM)] for s in order], axis=0)
+            scores = lax.dot_general(
+                q if g == 0 else q[group:], keys, (((1,), (1,)), ((), ())), preferred_element_type=jnp.float32
+            )
+            for i, s in enumerate(order):
+                key_doc = meta[cell * sources + s, pl.ds(g, 1), :]
+                key_pos = meta[cell * sources + s, pl.ds(2 + g, 1), :]
+                for slot in range(g, 2):
+                    row = (slot - g) * group
+                    block = scores[row:row + group, i * group:(i + 1) * group]
+                    if i:
+                        seen = jnp.where(key_pos < pos_line[slot], key_doc, -1.0) == doc[slot]
+                    else:
+                        seen = (key_doc == doc[slot]) & (key_pos <= pos[slot])
+                    parts[slot].append(jnp.where(seen, block, MASKED))
+        best = []
+        weights = []
+        sums = []
+        for slot in range(2):
+            top = functools.reduce(jnp.maximum, parts[slot])
+            top = jnp.broadcast_to(jnp.max(top, axis=1, keepdims=True), (group, group))
+            found = [jnp.exp2((one - top) * factor) for one in parts[slot]]
+            total = jnp.sum(functools.reduce(jnp.add, found), axis=1, keepdims=True)
+            best.append(to_lanes(top))
+            sums.append(to_lanes(jnp.broadcast_to(total, (group, group))))
+            weights.append([one.astype(jnp.bfloat16) for one in found])
+        outs = []
+        for g in range(2):
+            part = pl.ds(g * group, group)
+            vals = jnp.concatenate([kv[s, part, pl.ds(HEAD_DIM, HEAD_DIM)] for s in order], axis=0)
+            lines = [jnp.concatenate(weights[slot][g * sources:(g + 1) * sources], axis=1) for slot in range(g, 2)]
+            line = lines[0] if g else jnp.concatenate(lines, axis=0)
+            outs.append(jnp.dot(line, vals, preferred_element_type=jnp.float32))
+        return (outs[0][:group], outs[0][group:] + outs[1]), best, sums
 
     def o_copy(cc, ch, n):
         return remote(osend.at[n], obuf.at[cell, chip], o_send.at[n], o_recv.at[cell, chip], index(cc, ch, core))
@@ -203,7 +224,8 @@
         return remote(ssend.at[0], sbuf.at[cc, h], s_send.at[0], s_recv.at[cc, h], partner)
 
     def place_of(t):
-        return lax.rem(cell + 1 + t // heads, cells), lax.rem(chip + lax.rem(t, heads), heads)
+        cc = lax.rem(cell + 1 + t // heads, cells)
+        return cc, facing(cc, lax.rem(t, heads))
 
     def serve(t, carry):
         cc, ch = place_of(t)
@@ -219,12 +241,11 @@
             meta_arrival(home).wait_recv()
 
         pl.when(cc != cell)(arrive_meta)
+        outs, best, sums = attend(cc, ch, home)
         for slot in range(2):
-            q = qin[cc, ch, pl.ds(slot * group, group), :]
-            out, best, total = attend(q, home, slot)
-            osend[t, pl.ds(slot * group, group), :] = out.astype(jnp.bfloat16)
-            ssend[t, pl.ds(slot, 1), :] = best
-            ssend[t, pl.ds(2 + slot, 1), :] = total
+            osend[t, pl.ds(slot * group, group), :] = outs[slot].astype(jnp.bfloat16)
+            ssend[t, pl.ds(slot, 1), :] = best[slot]
+            ssend[t, pl.ds(2 + slot, 1), :] = sums[slot]
 
         def give():
             o_copy(cc, ch, t).start()
@@ -235,7 +256,7 @@
 
     lax.fori_loop(0, cells * heads, serve, 0)
 
-    own_turn = (cells - 1) * heads
+    own_turn = (cells - 1) * heads + chip
     obuf[cell, chip] = osend[own_turn]
     sbuf[cell, chip] = ssend[own_turn]
 
@@ -261,8 +282,7 @@
                 weight = to_rows(scale[cc] / total)
                 term = obuf[cc, h, part, :].astype(jnp.float32) * weight
                 mixed = term if mixed is None else mixed + term
-            mixed_ref[h, part, :] = mixed.astype(mixed_ref.dtype)
-        out_copy(h).start()
+            out_hbm[part, pl.ds(h * HEAD_DIM, HEAD_DIM)] = mixed.astype(out_hbm.dtype)
 
     for cc, ch, n in peers:
         q_copy(cc, ch, n).wait_send()
@@ -284,8 +304,6 @@
         return carry
 
     lax.fori_loop(0, cells * heads, drain, 0)
-    for h in range(heads):
-        out_copy(h).wait()
 
 
 def solution(mesh):
@@ -303,7 +321,7 @@
             functools.partial(attend_kernel, cells),
             out_shape=jax.ShapeDtypeStruct((rows, cols), bf16),
             in_specs=[pl.BlockSpec(memory_space=pl.ANY)] * 5,
-            out_specs=pl.BlockSpec(memory_space=pl.ANY),
+            out_specs=pl.BlockSpec(memory_space=pltpu.VMEM),
             scratch_shapes=[
                 pltpu.SMEM((1, 2), jnp.int32),
                 pltpu.VMEM(doc_rows.shape, jnp.int32),
@@ -312,7 +330,7 @@
                 pltpu.VMEM((heads, rows, 2 * HEAD_DIM), bf16),
                 pltpu.VMEM((cells, heads, rows, HEAD_DIM), bf16),
                 pltpu.VMEM((heads * CORES, rows, 2 * HEAD_DIM), bf16),
-                pltpu.VMEM((members, 4, group), jnp.int32),
+                pltpu.VMEM((members, 4, group), f32),
                 pltpu.VMEM((cells * heads, rows, HEAD_DIM), bf16),
                 pltpu.VMEM((cells * heads, 4, group), f32),
                 pltpu.VMEM((cells, heads, rows, HEAD_DIM), bf16),
@@ -336,9 +354,9 @@
                 dma((cells, heads)),
             ],
             compiler_params=pltpu.CompilerParams(
-                collective_id=0, has_side_effects=True, vmem_limit_bytes=60 * 1024 * 1024
+                collective_id=0, has_side_effects=True, vmem_limit_bytes=12 * 1024 * 1024
             ),
-        )(group_table, queries, keys, values, doc_rows)
+        )(*[pltpu.with_memory_space_constraint(one, pltpu.HBM) for one in (group_table, queries, keys, values, doc_rows)])
 
     in_specs = (P("blk", "head"), P("blk", "head"), P("blk", "head"), P("blk", None), P())
     return jax.shard_map(shards, mesh=mesh, in_specs=in_specs, out_specs=P("blk", "head"), check_vma=False)

time: 36.9 us -> 34.5 us (0.935)
  Pallas kernels: 35 us -> 33.7 us
  local copies, waits for them, and re-layouts: 1.67 us -> 0.71 us
    pallas_call x1, Pallas kernels: 35 us -> 33.7 us  [shards(): pl.pallas_call(functools.partial(attend_kernel, cells), out_shape=jax.Sha...]
    unnamed x1, local copies, waits for them, and re-layouts: 1.67 us -> 0.71 us
where the time goes in v3:
time: 34.5 us; the launch traced here: 34.4 us
  Pallas kernels  33.7 us (98%)
  local copies, waits for them, and re-layouts  0.71 us (2%)
    pallas_call x1, Pallas kernels, shards(): pl.pallas_call(functools.partial(attend_kernel, cells), out_shape=jax.Sha...  33.7 us
    unnamed x1, local copies, waits for them, and re-layouts  0.71 us

profile of v3, /device:TPU:0, one launch (start us, length us, event | category | flops | bytes accessed | tf_op | source)
XLA Modules:
  0.0 34.4 jit_solution(2518385211513824630)
XLA Ops:
  0.0 33.7 %shard_map.55 = bf16[256,512]{1,0:T(8,128)(2,1)S(1)} custom-call(s32[1,2]{1,0:T(1,128)} %table_hbm.1, bf16[256,512]{1,0:T(8,128)(2,1)} %q_hbm.1, bf16[256,512]{1,0:T(8,128)(2,1)} %k_hbm.1, bf16[256,512]{1,0:T(8,128)(2,1)} %v_hbm.1, s32[32,128]{1,0:T(8,128)} %bitcast.1), custom_call_target="tpu_custom_call" | custom-call | tf_op jit(solution)/shard_map/pallas_call | solution.py:320
  33.7 0.7 %copy.7 = bf16[256,512]{1,0:T(8,128)(2,1)} copy(bf16[256,512]{1,0:T(8,128)(2,1)S(1)} %shard_map.55) | data formatting | bytes 524288

commit v4 on v3

--- a/solution.py
+++ b/solution.py
@@ -16,7 +16,7 @@
 def attend_kernel(
     cells, table_hbm, q_hbm, k_hbm, v_hbm, doc_hbm, out_hbm,
     table_ref, doc_ref, mixed_ref, stage_q, stage_kv, qin, kv, meta, osend, ssend, obuf, sbuf,
-    small_sem, out_sem, load_q, load_kv, own_sem, q_send, q_recv, kv_send, kv_recv, fwd_send, m_send, m_recv, mf_send,
+    ready, small_sem, out_sem, load_q, load_kv, own_sem, q_send, q_recv, kv_send, kv_recv, fwd_send, m_send, m_recv, mf_send,
     o_send, o_recv, s_send, s_recv,
 ):
     rows, cols = q_hbm.shape
@@ -80,9 +80,33 @@
         other = lax.rem(cell + k, cells)
         for i in range(heads):
             peers.append((other, facing(other, i) ^ lax.rem(chip, 2), k * heads + i))
-    for cc, ch, _ in peers:
-        pl.semaphore_signal(barrier, inc=1, device_id={"blk": index(cc, ch, core)})
-    pl.semaphore_signal(barrier, inc=1, device_id={"blk": partner})
+    mates = [one for one in peers if one[2] < heads]
+    others = [one for one in peers if one[2] >= heads]
+    for cc, ch, _ in mates:
+        pl.semaphore_signal(barrier, inc=1, device_id={"blk": index(cc, ch, 0)})
+    for cc, ch, _ in others:
+        pl.semaphore_signal(barrier, inc=1, device_id={"blk": index(cc, ch, 1)})
+
+    def greet_partner():
+        pl.semaphore_signal(barrier, inc=1, device_id={"blk": partner})
+
+    pl.when(core == 1)(greet_partner)
+
+    def cell_here():
+        def hear():
+            pl.semaphore_wait(barrier, CORES * len(mates) + 1)
+            pl.semaphore_signal(ready.at[0], inc=1, device_id={"blk": partner})
+
+        pl.when(core == 0)(hear)
+        pl.when(core == 1)(lambda: pl.semaphore_wait(ready.at[0], 1))
+
+    def others_here():
+        def hear():
+            pl.semaphore_wait(barrier, CORES * len(others))
+            pl.semaphore_signal(ready.at[1], inc=1, device_id={"blk": partner})
+
+        pl.when(core == 1)(hear)
+        pl.when(core == 0)(lambda: pl.semaphore_wait(ready.at[1], 1))
 
     for one in small_loads:
         one.wait()
@@ -91,7 +115,7 @@
         own_group = table_ref[0, g]
         meta[me, pl.ds(g, 1), :] = doc_ref[pl.ds(own_group, 1), :].astype(jnp.float32)
         meta[me, pl.ds(2 + g, 1), :] = (own_group * group + within).astype(jnp.float32)
-    pl.semaphore_wait(barrier, len(peers) + 1)
+    cell_here()
 
     def remote(src, dst, ssem, rsem, target):
         return pltpu.make_async_remote_copy(
@@ -127,7 +151,7 @@
 
     near = [one for one in peers if one[2] < heads]
     far = [one for one in peers if one[2] >= heads]
-    for cc, ch, n in peers:
+    for cc, ch, n in near:
         meta_copy(cc, ch, n).start()
     meta_forward(chip).start()
     for pair in kv_loads:
@@ -140,6 +164,9 @@
     kv_forward(chip).start()
     for one in q_loads:
         one.wait()
+    others_here()
+    for cc, ch, n in far:
+        meta_copy(cc, ch, n).start()
     for cc, ch, n in far:
         q_copy(cc, ch, n).start()
     for cc, ch, n in near:
@@ -335,6 +362,7 @@
                 pltpu.VMEM((cells * heads, 4, group), f32),
                 pltpu.VMEM((cells, heads, rows, HEAD_DIM), bf16),
                 pltpu.VMEM((cells, heads, 4, group), f32),
+                pltpu.SemaphoreType.REGULAR((2,)),
                 dma((2,)),
                 dma((heads,)),
                 dma((heads,)),

time: 34.5 us -> 34 us (0.986)
  Pallas kernels: 33.7 us -> 33.1 us
    pallas_call x1, Pallas kernels: 33.7 us -> 33.1 us  [shards(): pl.pallas_call(functools.partial(attend_kernel, cells), out_shape=jax.Sha...]
where the time goes in v4:
time: 34 us; the launch traced here: 33.8 us
  Pallas kernels  33.1 us (97%)
  local copies, waits for them, and re-layouts  0.71 us (2%)
    pallas_call x1, Pallas kernels, shards(): pl.pallas_call(functools.partial(attend_kernel, cells), out_shape=jax.Sha...  33.1 us
    unnamed x1, local copies, waits for them, and re-layouts  0.71 us

profile of v4, /device:TPU:0, one launch (start us, length us, event | category | flops | bytes accessed | tf_op | source)
XLA Modules:
  0.0 33.8 jit_solution(2019473344846933754)
XLA Ops:
  0.0 33.1 %shard_map.55 = bf16[256,512]{1,0:T(8,128)(2,1)S(1)} custom-call(s32[1,2]{1,0:T(1,128)} %table_hbm.1, bf16[256,512]{1,0:T(8,128)(2,1)} %q_hbm.1, bf16[256,512]{1,0:T(8,128)(2,1)} %k_hbm.1, bf16[256,512]{1,0:T(8,128)(2,1)} %v_hbm.1, s32[32,128]{1,0:T(8,128)} %bitcast.1), custom_call_target="tpu_custom_call" | custom-call | tf_op jit(solution)/shard_map/pallas_call | solution.py:347
  33.1 0.7 %copy.7 = bf16[256,512]{1,0:T(8,128)(2,1)} copy(bf16[256,512]{1,0:T(8,128)(2,1)S(1)} %shard_map.55) | data formatting | bytes 524288

commit v5 on v4

--- a/solution.py
+++ b/solution.py
@@ -14,10 +14,10 @@
 
 
 def attend_kernel(
-    cells, table_hbm, q_hbm, k_hbm, v_hbm, doc_hbm, out_hbm,
-    table_ref, doc_ref, mixed_ref, stage_q, stage_kv, qin, kv, meta, osend, ssend, obuf, sbuf,
-    ready, small_sem, out_sem, load_q, load_kv, own_sem, q_send, q_recv, kv_send, kv_recv, fwd_send, m_send, m_recv, mf_send,
-    o_send, o_recv, s_send, s_recv,
+    cells, table_hbm, q_hbm, k_hbm, v_hbm, doc_hbm, out_ref,
+    table_ref, doc_ref, stage_q, stage_kv, qin, kv, meta, osend, ssend, obuf, sbuf, measure,
+    ready, small_sem, load_q, load_kv, own_sem, q_send, q_recv, kv_send, kv_recv, fwd_send, m_send, mf_send,
+    o_send, s_send, o_recv,
 ):
     rows, cols = q_hbm.shape
     heads = cols // HEAD_DIM
@@ -45,27 +45,29 @@
     def own_slot(ch, co):
         return ch * CORES + co
 
-    q_loads = [pltpu.make_async_copy(q_hbm.at[:, head_columns(h)], stage_q.at[h], load_q.at[h]) for h in range(heads)]
+    q_loads = [pltpu.make_async_copy(q_hbm.at[:, head_columns(h)], stage_q.at[h], load_q) for h in range(heads)]
     kv_loads = []
     for h in range(heads):
-        kv_loads.append((
-            pltpu.make_async_copy(k_hbm.at[:, head_columns(h)], stage_kv.at[h, :, pl.ds(0, HEAD_DIM)], load_kv.at[h, 0]),
-            pltpu.make_async_copy(v_hbm.at[:, head_columns(h)], stage_kv.at[h, :, pl.ds(HEAD_DIM, HEAD_DIM)], load_kv.at[h, 1]),
-        ))
-    own_kv = (
-        pltpu.make_async_copy(k_hbm.at[:, head_columns(chip)], kv.at[own_slot(chip, core), :, pl.ds(0, HEAD_DIM)], own_sem.at[0]),
-        pltpu.make_async_copy(v_hbm.at[:, head_columns(chip)], kv.at[own_slot(chip, core), :, pl.ds(HEAD_DIM, HEAD_DIM)], own_sem.at[1]),
-    )
-    own_q = pltpu.make_async_copy(q_hbm.at[:, head_columns(chip)], qin.at[cell, chip], own_sem.at[2])
+        for part, source in enumerate((k_hbm, v_hbm)):
+            place = stage_kv.at[h, :, pl.ds(part * HEAD_DIM, HEAD_DIM)]
+            kv_loads.append(pltpu.make_async_copy(source.at[:, head_columns(h)], place, load_kv))
+    own_kv = [
+        pltpu.make_async_copy(
+            source.at[:, head_columns(chip)],
+            kv.at[own_slot(chip, core), :, pl.ds(part * HEAD_DIM, HEAD_DIM)],
+            own_sem.at[0],
+        )
+        for part, source in enumerate((k_hbm, v_hbm))
+    ]
+    own_q = pltpu.make_async_copy(q_hbm.at[:, head_columns(chip)], qin.at[cell, chip], own_sem.at[1])
     small_loads = (
         pltpu.make_async_copy(table_hbm, table_ref, small_sem.at[0]),
         pltpu.make_async_copy(doc_hbm, doc_ref, small_sem.at[1]),
     )
     for one in small_loads:
         one.start()
-    for pair in kv_loads:
-        for one in pair:
-            one.start()
+    for one in kv_loads:
+        one.start()
     for one in own_kv:
         one.start()
     for one in q_loads:
@@ -122,65 +124,64 @@
             src_ref=src, dst_ref=dst, send_sem=ssem, recv_sem=rsem, device_id={"blk": target}
         )
 
-    def q_copy(cc, ch, n):
-        return remote(stage_q.at[ch], qin.at[cell, chip], q_send.at[n], q_recv.at[cell, chip], index(cc, ch, core))
-
-    def kv_copy(ch, n):
+    def q_copy(cc, ch):
+        return remote(stage_q.at[ch], qin.at[cell, chip], q_send, q_recv.at[cell, chip], index(cc, ch, core))
+
+    def kv_copy(ch):
         place = own_slot(chip, core)
-        return remote(stage_kv.at[ch], kv.at[place], kv_send.at[n], kv_recv.at[place], index(cell, ch, core))
+        return remote(stage_kv.at[ch], kv.at[place], kv_send, kv_recv.at[place], index(cell, ch, core))
 
     def kv_forward(ch):
         place = own_slot(ch, core)
-        return remote(kv.at[place], kv.at[place], fwd_send.at[ch], kv_recv.at[place], partner)
-
-    def meta_copy(cc, ch, n):
-        return remote(meta.at[me], meta.at[me], m_send.at[n], m_recv.at[me], index(cc, ch, core))
+        return remote(kv.at[place], kv.at[place], fwd_send, kv_recv.at[place], partner)
+
+    def near_meta(ch):
+        place = own_slot(chip, core)
+        return remote(meta.at[me], meta.at[me], m_send, kv_recv.at[place], index(cell, ch, core))
+
+    def far_meta(cc, ch):
+        return remote(meta.at[me], meta.at[me], m_send, q_recv.at[cell, chip], index(cc, ch, core))
 
     def meta_forward(ch):
         source = index(cell, ch, core)
-        return remote(meta.at[source], meta.at[source], mf_send.at[ch], m_recv.at[source], partner)
-
-    def q_arrival(cc, ch):
-        return remote(stage_q.at[0], qin.at[cc, ch], q_send.at[0], q_recv.at[cc, ch], partner)
+        return remote(meta.at[source], meta.at[source], mf_send, kv_recv.at[own_slot(ch, core)], partner)
+
+    def await_all(ref, sem):
+        pltpu.make_async_copy(ref, ref, sem).wait()
+
+    def await_rows(count, sem):
+        await_all(measure.at[pl.ds(0, count)], sem)
+
+    meta_rows = 2 * meta.shape[1]
 
     def kv_arrival(place):
-        return remote(kv.at[place], kv.at[place], fwd_send.at[0], kv_recv.at[place], partner)
-
-    def meta_arrival(source):
-        return remote(meta.at[source], meta.at[source], mf_send.at[0], m_recv.at[source], partner)
+        await_rows(2 * rows + meta_rows, kv_recv.at[place])
 
     near = [one for one in peers if one[2] < heads]
     far = [one for one in peers if one[2] >= heads]
     for cc, ch, n in near:
-        meta_copy(cc, ch, n).start()
+        near_meta(ch).start()
     meta_forward(chip).start()
-    for pair in kv_loads:
-        for one in pair:
-            one.wait()
+    await_all(stage_kv, load_kv)
     for cc, ch, n in near:
-        kv_copy(ch, n).start()
-    for one in own_kv:
-        one.wait()
+        kv_copy(ch).start()
+    await_all(kv.at[own_slot(chip, core)], own_sem.at[0])
     kv_forward(chip).start()
-    for one in q_loads:
-        one.wait()
+    await_all(stage_q, load_q)
     others_here()
     for cc, ch, n in far:
-        meta_copy(cc, ch, n).start()
+        far_meta(cc, ch).start()
     for cc, ch, n in far:
-        q_copy(cc, ch, n).start()
+        q_copy(cc, ch).start()
     for cc, ch, n in near:
-        q_copy(cc, ch, n).start()
+        q_copy(cc, ch).start()
     own_q.wait()
     for cc, ch, n in near:
-        kv_arrival(own_slot(ch, core)).wait_recv()
+        kv_arrival(own_slot(ch, core))
         kv_forward(ch).start()
-        meta_arrival(index(cell, ch, core)).wait_recv()
         meta_forward(ch).start()
     for i in range(heads):
-        ch = lax.rem(chip + i, heads)
-        kv_arrival(own_slot(ch, 1 - core)).wait_recv()
-        meta_arrival(index(cell, ch, 1 - core)).wait_recv()
+        kv_arrival(own_slot(lax.rem(chip + i, heads), 1 - core))
 
     sources = heads * CORES
     down = lax.broadcasted_iota(jnp.int32, (group, group), 0)
@@ -239,16 +240,10 @@
         return (outs[0][:group], outs[0][group:] + outs[1]), best, sums
 
     def o_copy(cc, ch, n):
-        return remote(osend.at[n], obuf.at[cell, chip], o_send.at[n], o_recv.at[cell, chip], index(cc, ch, core))
+        return remote(osend.at[n], obuf.at[cell, chip], o_send, o_recv.at[cell, chip], index(cc, ch, core))
 
     def s_copy(cc, ch, n):
-        return remote(ssend.at[n], sbuf.at[cell, chip], s_send.at[n], s_recv.at[cell, chip], index(cc, ch, core))
-
-    def o_arrival(cc, h):
-        return remote(osend.at[0], obuf.at[cc, h], o_send.at[0], o_recv.at[cc, h], partner)
-
-    def s_arrival(cc, h):
-        return remote(ssend.at[0], sbuf.at[cc, h], s_send.at[0], s_recv.at[cc, h], partner)
+        return remote(ssend.at[n], sbuf.at[cell, chip], s_send, o_recv.at[cell, chip], index(cc, ch, core))
 
     def place_of(t):
         cc = lax.rem(cell + 1 + t // heads, cells)
@@ -259,15 +254,8 @@
         home = index(cc, ch, core)
         other = home != me
 
-        def arrive():
-            q_arrival(cc, ch).wait_recv()
-
-        pl.when(other)(arrive)
-
-        def arrive_meta():
-            meta_arrival(home).wait_recv()
-
-        pl.when(cc != cell)(arrive_meta)
+        pl.when((cc == cell) & other)(lambda: await_rows(rows, q_recv.at[cc, ch]))
+        pl.when(cc != cell)(lambda: await_rows(rows + meta_rows, q_recv.at[cc, ch]))
         outs, best, sums = attend(cc, ch, home)
         for slot in range(2):
             osend[t, pl.ds(slot * group, group), :] = outs[slot].astype(jnp.bfloat16)
@@ -287,16 +275,9 @@
     obuf[cell, chip] = osend[own_turn]
     sbuf[cell, chip] = ssend[own_turn]
 
-    def out_copy(h):
-        return pltpu.make_async_copy(mixed_ref.at[h], out_hbm.at[:, head_columns(h)], out_sem.at[h])
-
     for h in range(heads):
         for cc in range(cells):
-            def arrive_partial():
-                o_arrival(cc, h).wait_recv()
-                s_arrival(cc, h).wait_recv()
-
-            pl.when((cell != cc) | (chip != h))(arrive_partial)
+            pl.when((cell != cc) | (chip != h))(lambda: await_rows(rows + meta_rows, o_recv.at[cc, h]))
         for slot in range(2):
             part = pl.ds(slot * group, group)
             tops = [sbuf[cc, h, pl.ds(slot, 1), :] for cc in range(cells)]
@@ -309,28 +290,16 @@
                 weight = to_rows(scale[cc] / total)
                 term = obuf[cc, h, part, :].astype(jnp.float32) * weight
                 mixed = term if mixed is None else mixed + term
-            out_hbm[part, pl.ds(h * HEAD_DIM, HEAD_DIM)] = mixed.astype(out_hbm.dtype)
-
-    for cc, ch, n in peers:
-        q_copy(cc, ch, n).wait_send()
-        meta_copy(cc, ch, n).wait_send()
-    for cc, ch, n in near:
-        kv_copy(ch, n).wait_send()
-    for ch in range(heads):
-        kv_forward(ch).wait_send()
-        meta_forward(ch).wait_send()
-
-    def drain(t, carry):
-        cc, ch = place_of(t)
-
-        def finish():
-            o_copy(cc, ch, t).wait_send()
-            s_copy(cc, ch, t).wait_send()
-
-        pl.when(index(cc, ch, core) != me)(finish)
-        return carry
-
-    lax.fori_loop(0, cells * heads, drain, 0)
+            out_ref[part, pl.ds(h * HEAD_DIM, HEAD_DIM)] = mixed.astype(out_ref.dtype)
+
+    sent = pl.ds(0, cells * heads - 1)
+    await_all(osend.at[sent], q_send)
+    await_all(meta.at[sent], m_send)
+    await_all(kv.at[pl.ds(0, heads - 1)], kv_send)
+    await_all(kv.at[pl.ds(0, heads)], fwd_send)
+    await_all(meta.at[pl.ds(0, heads)], mf_send)
+    await_all(osend.at[sent], o_send)
+    await_all(ssend.at[sent], s_send)
 
 
 def solution(mesh):
@@ -353,7 +322,6 @@
                 pltpu.SMEM((1, 2), jnp.int32),
                 pltpu.VMEM(doc_rows.shape, jnp.int32),
                 pltpu.VMEM((heads, rows, HEAD_DIM), bf16),
-                pltpu.VMEM((heads, rows, HEAD_DIM), bf16),
                 pltpu.VMEM((heads, rows, 2 * HEAD_DIM), bf16),
                 pltpu.VMEM((cells, heads, rows, HEAD_DIM), bf16),
                 pltpu.VMEM((heads * CORES, rows, 2 * HEAD_DIM), bf16),
@@ -362,23 +330,21 @@
                 pltpu.VMEM((cells * heads, 4, group), f32),
                 pltpu.VMEM((cells, heads, rows, HEAD_DIM), bf16),
                 pltpu.VMEM((cells, heads, 4, group), f32),
+                pltpu.VMEM((2 * (rows + 4), HEAD_DIM), bf16),
                 pltpu.SemaphoreType.REGULAR((2,)),
                 dma((2,)),
-                dma((heads,)),
-                dma((heads,)),
-                dma((heads, 2)),
-                dma((3,)),
-                dma((cells * heads,)),
+                dma,
+                dma,
+                dma((2,)),
+                dma,
                 dma((cells, heads)),
-                dma((heads,)),
+                dma,
                 dma((heads * CORES,)),
-                dma((heads,)),
-                dma((cells * heads,)),
-                dma((members,)),
-                dma((heads,)),
-                dma((cells * heads,)),
-                dma((cells, heads)),
-                dma((cells * heads,)),
+                dma,
+                dma,
+                dma,
+                dma,
+                dma,
                 dma((cells, heads)),
             ],
             compiler_params=pltpu.CompilerParams(

time: 34 us -> 33.1 us (0.974)
  Pallas kernels: 33.1 us -> 32.2 us
    pallas_call x1, Pallas kernels: 33.1 us -> 32.2 us  [shards(): pl.pallas_call(functools.partial(attend_kernel, cells), out_shape=jax.Sha...]
where the time goes in v5:
time: 33.1 us; the launch traced here: 32.9 us
  Pallas kernels  32.2 us (97%)
  local copies, waits for them, and re-layouts  0.71 us (2%)
    pallas_call x1, Pallas kernels, shards(): pl.pallas_call(functools.partial(attend_kernel, cells), out_shape=jax.Sha...  32.2 us
    unnamed x1, local copies, waits for them, and re-layouts  0.71 us

profile of v5, /device:TPU:0, one launch (start us, length us, event | category | flops | bytes accessed | tf_op | source)
XLA Modules:
  0.0 32.9 jit_solution(16334876052296224882)
XLA Ops:
  0.0 32.2 %shard_map.55 = bf16[256,512]{1,0:T(8,128)(2,1)S(1)} custom-call(s32[1,2]{1,0:T(1,128)} %table_hbm.1, bf16[256,512]{1,0:T(8,128)(2,1)} %q_hbm.1, bf16[256,512]{1,0:T(8,128)(2,1)} %k_hbm.1, bf16[256,512]{1,0:T(8,128)(2,1)} %v_hbm.1, s32[32,128]{1,0:T(8,128)} %bitcast.1), custom_call_target="tpu_custom_call" | custom-call | tf_op jit(solution)/shard_map/pallas_call | solution.py:316
  32.2 0.7 %copy.7 = bf16[256,512]{1,0:T(8,128)(2,1)} copy(bf16[256,512]{1,0:T(8,128)(2,1)S(1)} %shard_map.55) | data formatting | bytes 524288

commit v6 on v5

--- a/solution.py
+++ b/solution.py
@@ -33,8 +33,12 @@
 
     partner = index(cell, chip, 1 - core)
 
+    half = heads // 2
+    layer = chip // half
+    inner = layer == (lax.rem(cell + 1, cells) > cell).astype(jnp.int32)
+
     def facing(other, i):
-        return lax.rem(i + (heads // 2) * (other < cell).astype(jnp.int32), heads)
+        return lax.rem(i + half * (other < cell).astype(jnp.int32), heads)
 
     def head_columns(h):
         start = h * HEAD_DIM
@@ -245,9 +249,20 @@
     def s_copy(cc, ch, n):
         return remote(ssend.at[n], sbuf.at[cell, chip], s_send, o_recv.at[cell, chip], index(cc, ch, core))
 
+    cross_block = jnp.where(inner, 2, 3)
+    own_block = jnp.where(inner, 3, 2)
+
     def place_of(t):
-        cc = lax.rem(cell + 1 + t // heads, cells)
-        return cc, facing(cc, lax.rem(t, heads))
+        block, step = t // half, lax.rem(t, half)
+        is_cross, is_own = block == cross_block, block == own_block
+        far_block = block - (cross_block < block).astype(jnp.int32) - (own_block < block).astype(jnp.int32)
+        other = lax.rem(cell + 1 + far_block // 2, cells)
+        far_layer = lax.rem(far_block + (inner).astype(jnp.int32), 2)
+        far_chip = facing(other, far_layer * half + step)
+        own_chip = layer * half + lax.rem(lax.rem(chip, half) + 1 + step, half)
+        near_chip = jnp.where(is_own, own_chip, (1 - layer) * half + step)
+        near_cell = is_cross | is_own
+        return jnp.where(near_cell, cell, other), jnp.where(near_cell, near_chip, far_chip)
 
     def serve(t, carry):
         cc, ch = place_of(t)
@@ -271,7 +286,7 @@
 
     lax.fori_loop(0, cells * heads, serve, 0)
 
-    own_turn = (cells - 1) * heads + chip
+    own_turn = own_block * half + half - 1
     obuf[cell, chip] = osend[own_turn]
     sbuf[cell, chip] = ssend[own_turn]
 

time: 33.1 us -> 30.9 us (0.934)
  Pallas kernels: 32.2 us -> 29.8 us
    pallas_call x1, Pallas kernels: 32.2 us -> 29.8 us  [shards(): pl.pallas_call(functools.partial(attend_kernel, cells), out_shape=jax.Sha...]
where the time goes in v6:
time: 30.9 us; the launch traced here: 30.6 us
  Pallas kernels  29.8 us (96%)
  local copies, waits for them, and re-layouts  0.71 us (2%)
    pallas_call x1, Pallas kernels, shards(): pl.pallas_call(functools.partial(attend_kernel, cells), out_shape=jax.Sha...  29.8 us
    unnamed x1, local copies, waits for them, and re-layouts  0.71 us

profile of v6, /device:TPU:0, one launch (start us, length us, event | category | flops | bytes accessed | tf_op | source)
XLA Modules:
  0.0 30.6 jit_solution(9615844129158875888)
XLA Ops:
  0.0 29.8 %shard_map.55 = bf16[256,512]{1,0:T(8,128)(2,1)S(1)} custom-call(s32[1,2]{1,0:T(1,128)} %table_hbm.1, bf16[256,512]{1,0:T(8,128)(2,1)} %q_hbm.1, bf16[256,512]{1,0:T(8,128)(2,1)} %k_hbm.1, bf16[256,512]{1,0:T(8,128)(2,1)} %v_hbm.1, s32[32,128]{1,0:T(8,128)} %bitcast.1), custom_call_target="tpu_custom_call" | custom-call | tf_op jit(solution)/shard_map/pallas_call | solution.py:331
  29.8 0.7 %copy.7 = bf16[256,512]{1,0:T(8,128)(2,1)} copy(bf16[256,512]{1,0:T(8,128)(2,1)S(1)} %shard_map.55) | data formatting | bytes 524288

commit v7 on v6

--- a/solution.py
+++ b/solution.py
@@ -290,7 +290,8 @@
     obuf[cell, chip] = osend[own_turn]
     sbuf[cell, chip] = ssend[own_turn]
 
-    for h in range(heads):
+    for i in range(heads):
+        h = lax.rem(layer * half + i, heads)
         for cc in range(cells):
             pl.when((cell != cc) | (chip != h))(lambda: await_rows(rows + meta_rows, o_recv.at[cc, h]))
         for slot in range(2):
@@ -305,7 +306,7 @@
                 weight = to_rows(scale[cc] / total)
                 term = obuf[cc, h, part, :].astype(jnp.float32) * weight
                 mixed = term if mixed is None else mixed + term
-            out_ref[part, pl.ds(h * HEAD_DIM, HEAD_DIM)] = mixed.astype(out_ref.dtype)
+            out_ref[part, head_columns(h)] = mixed.astype(out_ref.dtype)
 
     sent = pl.ds(0, cells * heads - 1)
     await_all(osend.at[sent], q_send)

time: 30.9 us -> 30.7 us (level)
  no operation moved by 1% of the time
where the time goes in v7:
time: 30.7 us; the launch traced here: 30.6 us
  Pallas kernels  29.8 us (97%)
  local copies, waits for them, and re-layouts  0.71 us (2%)
    pallas_call x1, Pallas kernels, shards(): pl.pallas_call(functools.partial(attend_kernel, cells), out_shape=jax.Sha...  29.8 us
    unnamed x1, local copies, waits for them, and re-layouts  0.71 us

profile of v7, /device:TPU:0, one launch (start us, length us, event | category | flops | bytes accessed | tf_op | source)
XLA Modules:
  0.0 30.6 jit_solution(7672026080747196296)
XLA Ops:
  0.0 29.8 %shard_map.55 = bf16[256,512]{1,0:T(8,128)(2,1)S(1)} custom-call(s32[1,2]{1,0:T(1,128)} %table_hbm.1, bf16[256,512]{1,0:T(8,128)(2,1)} %q_hbm.1, bf16[256,512]{1,0:T(8,128)(2,1)} %k_hbm.1, bf16[256,512]{1,0:T(8,128)(2,1)} %v_hbm.1, s32[32,128]{1,0:T(8,128)} %bitcast.1), custom_call_target="tpu_custom_call" | custom-call | tf_op jit(solution)/shard_map/pallas_call | solution.py:332
  29.8 0.7 %copy.7 = bf16[256,512]{1,0:T(8,128)(2,1)} copy(bf16[256,512]{1,0:T(8,128)(2,1)S(1)} %shard_map.55) | data formatting | bytes 524288

commit v8 on v7

--- a/solution.py
+++ b/solution.py
@@ -278,8 +278,8 @@
             ssend[t, pl.ds(2 + slot, 1), :] = sums[slot]
 
         def give():
+            s_copy(cc, ch, t).start()
             o_copy(cc, ch, t).start()
-            s_copy(cc, ch, t).start()
 
         pl.when(other)(give)
         return carry

time: 30.7 us -> 30.7 us (level)
  no operation moved by 1% of the time
where the time goes in v8:
time: 30.7 us; the launch traced here: 30.6 us
  Pallas kernels  29.8 us (97%)
  local copies, waits for them, and re-layouts  0.71 us (2%)
    pallas_call x1, Pallas kernels, shards(): pl.pallas_call(functools.partial(attend_kernel, cells), out_shape=jax.Sha...  29.8 us
    unnamed x1, local copies, waits for them, and re-layouts  0.71 us

profile of v8, /device:TPU:0, one launch (start us, length us, event | category | flops | bytes accessed | tf_op | source)
XLA Modules:
  0.0 30.6 jit_solution(5495577291192794363)
XLA Ops:
  0.0 29.8 %shard_map.55 = bf16[256,512]{1,0:T(8,128)(2,1)S(1)} custom-call(s32[1,2]{1,0:T(1,128)} %table_hbm.1, bf16[256,512]{1,0:T(8,128)(2,1)} %q_hbm.1, bf16[256,512]{1,0:T(8,128)(2,1)} %k_hbm.1, bf16[256,512]{1,0:T(8,128)(2,1)} %v_hbm.1, s32[32,128]{1,0:T(8,128)} %bitcast.1), custom_call_target="tpu_custom_call" | custom-call | tf_op jit(solution)/shard_map/pallas_call | solution.py:332
  29.8 0.7 %copy.7 = bf16[256,512]{1,0:T(8,128)(2,1)} copy(bf16[256,512]{1,0:T(8,128)(2,1)S(1)} %shard_map.55) | data formatting | bytes 524288

commit v9 on v8

--- a/solution.py
+++ b/solution.py
@@ -16,7 +16,7 @@
 def attend_kernel(
     cells, table_hbm, q_hbm, k_hbm, v_hbm, doc_hbm, out_ref,
     table_ref, doc_ref, stage_q, stage_kv, qin, kv, meta, osend, ssend, obuf, sbuf, measure,
-    ready, small_sem, load_q, load_kv, own_sem, q_send, q_recv, kv_send, kv_recv, fwd_send, m_send, mf_send,
+    ready, small_sem, load_q, load_kv, own_sem, q_send, q_recv, kv_send, kv_recv, m_send,
     o_send, s_send, o_recv,
 ):
     rows, cols = q_hbm.shape
@@ -93,10 +93,7 @@
     for cc, ch, _ in others:
         pl.semaphore_signal(barrier, inc=1, device_id={"blk": index(cc, ch, 1)})
 
-    def greet_partner():
-        pl.semaphore_signal(barrier, inc=1, device_id={"blk": partner})
-
-    pl.when(core == 1)(greet_partner)
+    pl.semaphore_signal(barrier, inc=1, device_id={"blk": partner})
 
     def cell_here():
         def hear():
@@ -108,7 +105,7 @@
 
     def others_here():
         def hear():
-            pl.semaphore_wait(barrier, CORES * len(others))
+            pl.semaphore_wait(barrier, CORES * len(others) + 1)
             pl.semaphore_signal(ready.at[1], inc=1, device_id={"blk": partner})
 
         pl.when(core == 1)(hear)
@@ -137,7 +134,7 @@
 
     def kv_forward(ch):
         place = own_slot(ch, core)
-        return remote(kv.at[place], kv.at[place], fwd_send, kv_recv.at[place], partner)
+        return remote(kv.at[place], kv.at[place], kv_send, kv_recv.at[place], partner)
 
     def near_meta(ch):
         place = own_slot(chip, core)
@@ -148,7 +145,7 @@
 
     def meta_forward(ch):
         source = index(cell, ch, core)
-        return remote(meta.at[source], meta.at[source], mf_send, kv_recv.at[own_slot(ch, core)], partner)
+        return remote(meta.at[source], meta.at[source], m_send, kv_recv.at[own_slot(ch, core)], partner)
 
     def await_all(ref, sem):
         pltpu.make_async_copy(ref, ref, sem).wait()
@@ -310,10 +307,8 @@
 
     sent = pl.ds(0, cells * heads - 1)
     await_all(osend.at[sent], q_send)
-    await_all(meta.at[sent], m_send)
-    await_all(kv.at[pl.ds(0, heads - 1)], kv_send)
-    await_all(kv.at[pl.ds(0, heads)], fwd_send)
-    await_all(meta.at[pl.ds(0, heads)], mf_send)
+    await_all(meta.at[pl.ds(0, cells * heads - 1 + heads)], m_send)
+    await_all(kv.at[pl.ds(0, 2 * heads - 1)], kv_send)
     await_all(osend.at[sent], o_send)
     await_all(ssend.at[sent], s_send)
 
@@ -359,8 +354,6 @@
                 dma,
                 dma,
                 dma,
-                dma,
-                dma,
                 dma((cells, heads)),
             ],
             compiler_params=pltpu.CompilerParams(

time: 30.7 us -> 30.7 us (level)
  no operation moved by 1% of the time
where the time goes in v9:
time: 30.7 us; the launch traced here: 30.5 us
  Pallas kernels  29.8 us (97%)
  local copies, waits for them, and re-layouts  0.71 us (2%)
    pallas_call x1, Pallas kernels, shards(): pl.pallas_call(functools.partial(attend_kernel, cells), out_shape=jax.Sha...  29.8 us
    unnamed x1, local copies, waits for them, and re-layouts  0.71 us

profile of v9, /device:TPU:0, one launch (start us, length us, event | category | flops | bytes accessed | tf_op | source)
XLA Modules:
  0.0 30.5 jit_solution(9363280292156444332)
XLA Ops:
  0.0 29.8 %shard_map.55 = bf16[256,512]{1,0:T(8,128)(2,1)S(1)} custom-call(s32[1,2]{1,0:T(1,128)} %table_hbm.1, bf16[256,512]{1,0:T(8,128)(2,1)} %q_hbm.1, bf16[256,512]{1,0:T(8,128)(2,1)} %k_hbm.1, bf16[256,512]{1,0:T(8,128)(2,1)} %v_hbm.1, s32[32,128]{1,0:T(8,128)} %bitcast.1), custom_call_target="tpu_custom_call" | custom-call | tf_op jit(solution)/shard_map/pallas_call | solution.py:327
  29.8 0.7 %copy.7 = bf16[256,512]{1,0:T(8,128)(2,1)} copy(bf16[256,512]{1,0:T(8,128)(2,1)S(1)} %shard_map.55) | data formatting | bytes 524288

commit v10 on v9

--- a/solution.py
+++ b/solution.py
@@ -85,7 +85,8 @@
     for k in range(1, cells):
         other = lax.rem(cell + k, cells)
         for i in range(heads):
-            peers.append((other, facing(other, i) ^ lax.rem(chip, 2), k * heads + i))
+            turned = jnp.where(inner, (i % 2) * half + i // 2, i)
+            peers.append((other, facing(other, turned) ^ lax.rem(chip, 2), k * heads + i))
     mates = [one for one in peers if one[2] < heads]
     others = [one for one in peers if one[2] >= heads]
     for cc, ch, _ in mates:

time: 30.7 us -> 30.8 us (level)
  no operation moved by 1% of the time
where the time goes in v10:
time: 30.8 us; the launch traced here: 30.6 us
  Pallas kernels  29.9 us (97%)
  local copies, waits for them, and re-layouts  0.71 us (2%)
    pallas_call x1, Pallas kernels, shards(): pl.pallas_call(functools.partial(attend_kernel, cells), out_shape=jax.Sha...  29.9 us
    unnamed x1, local copies, waits for them, and re-layouts  0.71 us

profile of v10, /device:TPU:0, one launch (start us, length us, event | category | flops | bytes accessed | tf_op | source)
XLA Modules:
  0.0 30.6 jit_solution(12100908661267950652)
XLA Ops:
  0.0 29.9 %shard_map.55 = bf16[256,512]{1,0:T(8,128)(2,1)S(1)} custom-call(s32[1,2]{1,0:T(1,128)} %table_hbm.1, bf16[256,512]{1,0:T(8,128)(2,1)} %q_hbm.1, bf16[256,512]{1,0:T(8,128)(2,1)} %k_hbm.1, bf16[256,512]{1,0:T(8,128)(2,1)} %v_hbm.1, s32[32,128]{1,0:T(8,128)} %bitcast.1), custom_call_target="tpu_custom_call" | custom-call | tf_op jit(solution)/shard_map/pallas_call | solution.py:328
  29.9 0.7 %copy.7 = bf16[256,512]{1,0:T(8,128)(2,1)} copy(bf16[256,512]{1,0:T(8,128)(2,1)S(1)} %shard_map.55) | data formatting | bytes 524288
